TPU v7x, 512 devices: a 8x2x16 block of a 8x8x16 slice. The times are simulated.
512 devices in a mesh: cfg: 2 (over y), site: 16 (over z), vec: 8 (over x), tslice: 2 (over core).
Axes of the slice: x: 8, y: 2, z: 16, core: 2. Of those that a mesh axis runs over, the one named last changes fastest.
The devices are a block of a 8x8x16 slice.
Arguments:
- eigvecs: float32 [4, 2, 3, 384, 16, 512], P(('cfg', 'tslice'), None, None, 'vec', 'site'), parts along dimension 0, may hold values from -1 to 1
- links: float32 [4, 3, 2, 3, 3, 16, 512], P(('cfg', 'tslice'), None, None, None, None, 'site'), parts along dimension 0, may hold values from -1 to 1, as said below
- peramb: bfloat16 [4, 32, 4, 2, 384, 384], P(('cfg', 'tslice'), 'site', None, None, 'vec'), parts along dimension 0, may hold values from -0.21875 to 0.21875
- block_owner: int32 [8], replicated, may hold values from 0 to 7, each once
- momenta: int32 [2, 3], replicated, may hold values from -2 to 2, as said below
Outputs:
- projected: bfloat16 [4, 32, 4, 2, 2, 384, 384], P(('cfg', 'tslice'), 'site', None, None, None, 'vec'), parts along dimension 0
There are 2 independent parts, one for each index of `cfg`. A program takes and returns all parts, laid end to end along the dimension named above; an argument that names none is the same for every part. Nothing has to cross between parts.
Inputs may be any that keep to these rules, and one draw needn't show every extreme that they name: Block b of eigvecs holds the eigenvectors numbered from block_owner[b] * 48 on; every block number appears once. `momenta`: every component is -2, -1, 1 or 2, never zero. `links`: every 3 x 3 link matrix is unitary.
All inputs are finite; a program needn't handle non-finite values.
Results may differ from a plain program's by a relative error of at most 0.0065.
Values may be sent and summed in bfloat16 or wider, within the bound.
A program may use at most 64 MiB of HBM per device.

v0:
```python
import math

import jax
import jax.numpy as jnp
from jax import lax
from jax.sharding import PartitionSpec as P

LX = 32
LY = 16


two_pi = 2.0 * math.pi


def from_behind(block, axis, distance):
    devices = range(lax.axis_size(axis))
    route = [((i - distance) % len(devices), i) for i in devices]
    return lax.ppermute(block, axis, route)


def with_halo(block, sides, width):
    for axis, dim in sides:
        count = lax.axis_size(axis)
        forward = [(i, i + 1) for i in range(count - 1)]
        forward.append((count - 1, 0))
        backward = [(target, source) for source, target in forward]
        low = lax.ppermute(
            lax.slice_in_dim(block, block.shape[dim] - width, None, axis=dim), axis, forward
        )
        high = lax.ppermute(lax.slice_in_dim(block, 0, width, axis=dim), axis, backward)
        block = jnp.concatenate([low, block, high], axis=dim)
    return block


def scatter_axes(shard, axes, dim):
    if not axes:
        return shard
    nearer = lax.psum_scatter(shard, axes[0], scatter_dimension=dim, tiled=True)
    return scatter_axes(nearer, axes[1:], dim)


def in_order(blocks, dim):
    dims = list(blocks.shape[1:])
    dims[dim] *= blocks.shape[0]
    return jnp.moveaxis(blocks, 0, dim).reshape(dims)


def gather_in_order(shard, axes, sequence):
    blocks = shard[None]
    for k in sequence:
        blocks = lax.all_gather(blocks, axes[k], axis=0, tiled=True)
    block = [lax.axis_size(axes[k]) for k in reversed(sequence)]
    blocks = blocks.reshape(*block, *shard.shape)
    turned = sorted(range(len(sequence)), key=lambda place: sequence[len(sequence) - 1 - place])
    return blocks.transpose(*turned, *range(len(sequence), blocks.ndim)).reshape(-1, *shard.shape)


def gather_axes(shard, axes, sequence, dim):
    return in_order(gather_in_order(shard, axes, sequence), dim)


def along(field, direction, sense):
    width = field.shape[-1]
    column = lax.broadcasted_iota(jnp.int32, (width,), 0) % LX
    if direction == 0:
        if sense > 0:
            return jnp.where(column == LX - 1, jnp.roll(field, LX - 1, -1), jnp.roll(field, -1, -1))
        return jnp.where(column == 0, jnp.roll(field, 1 - LX, -1), jnp.roll(field, 1, -1))
    return jnp.roll(field, -sense * LX, -1)


def link_times(link_re, link_im, field_re, field_im, dagger):
    result_re = []
    result_im = []
    for target in range(3):
        summed_re = jnp.zeros_like(field_re[0])
        summed_im = jnp.zeros_like(field_re[0])
        for source in range(3):
            if dagger:
                entry_re = link_re[source, target][None]
                entry_im = -link_im[source, target][None]
            else:
                entry_re = link_re[target, source][None]
                entry_im = link_im[target, source][None]
            summed_re = summed_re + entry_re * field_re[source] - entry_im * field_im[source]
            summed_im = summed_im + entry_re * field_im[source] + entry_im * field_re[source]
        result_re.append(summed_re)
        result_im.append(summed_im)
    return (jnp.stack(result_re), jnp.stack(result_im))


def chebyshev(initial, operate):
    current = operate(initial)
    following = 2.0 * operate(current) - initial
    return following


def phase_angle(momenta, across, upward, depth, extent):
    return two_pi * (
        (momenta[:, 0, None, None] * across[None]).astype(jnp.float32) / LX
        + (momenta[:, 1, None, None] * upward[None]).astype(jnp.float32) / LY
        + (momenta[:, 2, None, None] * depth[None]).astype(jnp.float32) / extent
    )


def per_device(eigvecs, links, peramb, block_owner, momenta):
    vectors = eigvecs[0]
    links_here = links[0]
    block = vectors.shape[2]
    layers = vectors.shape[3]
    plane = vectors.shape[4]
    site_count = lax.axis_size("site")
    group_count = lax.axis_size("vec")
    site_rank = lax.axis_index("site")
    group_rank = lax.axis_index("vec")
    portion = plane // group_count
    top_plane = links_here[2, :, :, :, layers - 1 :, :]
    below = from_behind(top_plane, "site", 1)
    behind_links = jnp.concatenate([below, links_here[2, :, :, :, : layers - 1, :]], axis=3)
    back_links = []
    for direction in range(2):
        back_links.append(
            (
                along(links_here[direction, 0], direction, -1),
                along(links_here[direction, 1], direction, -1),
            )
        )
    back_links.append((behind_links[0], behind_links[1]))

    def operate(field):
        padded = with_halo(field, (("site", 3),), 1)
        total_re = jnp.zeros_like(field[0])
        total_im = jnp.zeros_like(field[0])
        for direction in range(3):
            if direction < 2:
                ahead = along(field, direction, 1)
                behind = along(field, direction, -1)
            else:
                ahead = padded[:, :, :, 2:]
                behind = padded[:, :, :, :-2]
            forward = link_times(
                links_here[direction, 0], links_here[direction, 1], ahead[0], ahead[1], False
            )
            backward = link_times(
                back_links[direction][0], back_links[direction][1], behind[0], behind[1], True
            )
            total_re = total_re + forward[0] + backward[0]
            total_im = total_im + forward[1] + backward[1]
        return jnp.stack([total_re, total_im]) * (-1.0 / 6.0)

    filtered = chebyshev(vectors, operate).astype(jnp.bfloat16)
    received = lax.all_to_all(filtered, "vec", split_axis=4, concat_axis=2, tiled=True)
    grouped = received.reshape(2, 3, group_count, block, layers, portion)
    ranks = jnp.arange(group_count, dtype=jnp.int32)
    inverse = jnp.sum(
        ranks[:, None] * (block_owner[:, None] == ranks[None, :]).astype(jnp.int32), axis=0
    )
    ordered = jnp.take(grouped, inverse, axis=2).reshape(2, 3, group_count * block, layers, portion)
    nvec = group_count * block
    flat = group_rank * portion + lax.broadcasted_iota(jnp.int32, (layers, portion), 1)
    depth = site_rank * layers + lax.broadcasted_iota(jnp.int32, (layers, portion), 0)
    theta = phase_angle(momenta, flat % LX, flat // LX, depth, layers * site_count)
    values = ordered.astype(jnp.float32)
    cosine = jnp.cos(theta)[:, None, None]
    sine = jnp.sin(theta)[:, None, None]
    shift_re = cosine * values[0] + sine * values[1]
    shift_im = cosine * values[1] - sine * values[0]
    shifted = jnp.stack([shift_re, shift_im], axis=1).astype(jnp.bfloat16)
    products = jnp.einsum(
        "acizs,pbckzs->aipbk", ordered, shifted, preferred_element_type=jnp.float32
    )
    real = products[0, :, :, 0] + products[1, :, :, 1]
    imag = products[0, :, :, 1] - products[1, :, :, 0]
    momentum_count = momenta.shape[0]
    partial_sum = jnp.stack([real, imag], axis=2).reshape(nvec, momentum_count * 2 * nvec)
    tau = peramb[0]
    tau_rows = tau.reshape(-1, nvec)
    mine = scatter_axes(partial_sum, ("site", "vec"), 1).astype(jnp.bfloat16)
    joined = jnp.dot(
        tau_rows, gather_axes(mine, ("site", "vec"), (0, 1), 1), preferred_element_type=jnp.float32
    )
    sinks = tau.shape[0]
    spins = tau.shape[1]
    layout = joined.reshape(sinks, spins, 2, block, momentum_count, 2, nvec)
    real_part = layout[:, :, 0, :, :, 0] - layout[:, :, 1, :, :, 1]
    imag_part = layout[:, :, 0, :, :, 1] + layout[:, :, 1, :, :, 0]
    stacked = jnp.stack([real_part, imag_part], axis=0)
    result = jnp.transpose(stacked, (1, 2, 4, 0, 3, 5))
    return result[None].astype(jnp.bfloat16)


def solution(mesh):
    placed = (
        P(("cfg", "tslice"), None, None, "vec", "site", None),
        P(("cfg", "tslice"), None, None, None, None, "site", None),
        P(("cfg", "tslice"), "site", None, None, "vec", None),
        P(),
        P(),
    )
    return jax.shard_map(
        per_device,
        mesh=mesh,
        in_specs=placed,
        out_specs=P(("cfg", "tslice"), "site", None, None, None, "vec", None),
        check_vma=False,
    )
```

profile of v0, /device:TPU:80, one launch (start us, length us, event | category | flops | bytes accessed | tf_op | source)
XLA Modules:
  0.0 349.1 jit_solution(15257638496948450421)
XLA Ops:
  6.6 1.2 copy.365
  7.7 6.0 %collective-permute-start.2 = (f32[2,3,48,1,512]{4,2,3,1,0:T(8,128)S(1)}, f32[2,3,48,1,512]{4,2,3,1,0:T(8,128)S(1)}, u32[]{:S(2)}, u32[]{:S(2)}) collective-permute-start(f32[2,3,48,1,512]{4,2,3,1,0:T(8,128)S(1)} %bitcast.1146), channel_id=1, source_target_pairs={{0,16},{16,32},{32,48},{48,64},{64,80},{80,96},{96,112},{112,128},... | collective-permute-start | bytes 1769480 | tf_op jit(solution)/shard_map/ppermute | solution.py:27
  13.8 39.9 %collective-permute-start = (f32[2,3,48,1,512]{4,2,3,1,0:T(8,128)S(1)}, f32[2,3,48,1,512]{4,2,3,1,0:T(8,128)S(1)}, u32[]{:S(2)}, u32[]{:S(2)}) collective-permute-start(f32[2,3,48,1,512]{4,2,3,1,0:T(8,128)S(1)} %bitcast.1147), channel_id=1, source_target_pairs={{16,0},{32,16},{48,32},{64,48},{80,64},{96,80},{112,96},{128,112},... | collective-permute-start | bytes 1769480 | tf_op jit(solution)/shard_map/ppermute | solution.py:30
  54.4 1.9 collective-permute-start.1
  64.6 0.8 fusion.146
  65.4 0.8 fusion.149
  66.1 0.8 fusion.144
  67.2 1.2 fusion.148
  68.4 1.2 fusion.145
  70.9 1.5 slice_reduce_fusion.1
  72.4 1.4 fusion.151
  73.8 0.9 fusion.92
  74.7 0.9 fusion.104
  75.7 1.0 broadcast_select_fusion.1
  77.1 1.9 maximum_select_fusion
  83.3 0.8 subtract_bitcast_fusion.25
  84.2 0.8 subtract_bitcast_fusion.29
  85.0 0.8 subtract_bitcast_fusion.27
  85.8 0.8 subtract_bitcast_fusion.28
  87.9 1.3 broadcast_in_dim.50
  89.2 1.3 broadcast_in_dim.51
  94.5 5.2 %collective-permute-start.3 = (f32[2,3,48,1,512]{4,2,1,3,0:T(8,128)S(1)}, f32[2,3,48,1,512]{4,2,1,3,0:T(8,128)S(1)}, u32[]{:S(2)}, u32[]{:S(2)}) collective-permute-start(f32[2,3,48,1,512]{4,2,1,3,0:T(8,128)S(1)} %get-tuple-element.111), channel_id=1, source_target_pairs={{16,0},{32,16},{48,32},{64,48},{80,64},{96,80},{112,96},{128,112},... | collective-permute-start | bytes 1769480 | tf_op jit(solution)/shard_map/ppermute | solution.py:30
  99.6 2.1 collective-permute-start.4
  107.1 4.6 %collective-permute-done.3 = f32[2,3,48,1,512]{4,2,1,3,0:T(8,128)S(1)} collective-permute-done((f32[2,3,48,1,512]{4,2,1,3,0:T(8,128)S(1)}, f32[2,3,48,1,512]{4,2,1,3,0:T(8,128)S(1)}, u32[]{:S(2)}, u32[]{:S(2)}) %collective-permute-start.3) | collective-permute-done | bytes 589856 | tf_op jit(solution)/shard_map/ppermute | solution.py:30
  112.0 5.1 %collective-permute-done.4 = f32[2,3,48,1,512]{4,2,1,3,0:T(8,128)S(1)} collective-permute-done((f32[2,3,48,1,512]{4,2,1,3,0:T(8,128)S(1)}, f32[2,3,48,1,512]{4,2,1,3,0:T(8,128)S(1)}, u32[]{:S(2)}, u32[]{:S(2)}) %collective-permute-start.4) | collective-permute-done | bytes 589856 | tf_op jit(solution)/shard_map/ppermute | solution.py:27
  117.7 0.9 copy-done.1
  119.5 1.9 reshape.32232
  121.4 7.3 %all-to-all-start = ((bf16[8,2,9216]{2,1,0:T(2,128)(2,1)}), bf16[8,2,9216]{2,1,0:T(2,128)(2,1)S(1)}, u32[]{:S(2)}, u32[]{:S(2)}) async-start(bf16[8,2,9216]{2,1,0:T(2,128)(2,1)} %reshape.32232), calls=%async_computation | async-start | bytes 589824 | tf_op jit(solution)/shard_map/all_to_all | solution.py:152
  129.0 10.6 %all-to-all-done = bf16[8,2,9216]{2,1,0:T(2,128)(2,1)S(1)} async-done(((bf16[8,2,9216]{2,1,0:T(2,128)(2,1)}), bf16[8,2,9216]{2,1,0:T(2,128)(2,1)S(1)}, u32[]{:S(2)}, u32[]{:S(2)}) %all-to-all-start) | async-done | bytes 294944 | tf_op jit(solution)/shard_map/all_to_all | solution.py:152
  139.6 1.4 reshape.32233
  141.0 1.0 copy.319
  144.5 0.8 convolution_bitcast_fusion.1
  145.8 1.6 copy.324
  147.5 62.6 %reduce-scatter.4.cloned.1.call-done = f32[384,96]{0,1:T(8,128)} async-done(((f32[384,1536]{0,1:T(8,128)}), f32[384,96]{0,1:T(8,128)}) %reduce-scatter.4.cloned.1.call-update) | async-done | bytes 147472 | tf_op jit(solution)/shard_map/reduce_scatter | solution.py:38
  210.1 20.2 %fusion = f32[384,16]{0,1:T(8,128)S(1)} fusion(f32[384,96]{0,1:T(8,128)} %reduce-scatter.4.cloned.1.call-done), kind=kCustom, calls=%all-reduce-scatter | all-reduce-scatter fusion | flops 49153 | bytes 174080
  230.3 2.4 collective-permute-start.5
  232.7 3.0 collective-permute-start.6
  235.7 1.3 dynamic-slice.4
  238.0 28.3 %all-gather = bf16[6144,12]{0,1:T(8,128)(2,1)S(1)} all-gather(bf16[384,12]{0,1:T(8,128)(2,1)S(1)} %dynamic-slice_convert_fusion), channel_id=2, replica_groups=mesh['cfg'=2,'site'=16,'vec'=8,'tslice'=2] {'site'}, dimensions={0}, use_global_device_ids=true | all-gather | bytes 156672 | tf_op jit(solution)/shard_map/all_gather | solution.py:51
  267.1 44.1 %all-gather.3.cloned.1.call-done = bf16[128,384,12]{1,0,2:T(8,128)(2,1)} async-done(((bf16[16,384,12]{1,0,2:T(8,128)(2,1)}), bf16[128,384,12]{1,0,2:T(8,128)(2,1)}) %all-gather.3.cloned.1.call-update) | async-done | bytes 1179664 | tf_op jit(solution)/shard_map/all_gather | solution.py:51
  311.2 1.5 copy.364
  312.8 1.9 copy.326
  314.7 2.3 reshape.32210
  316.9 3.6 %convolution_bitcast_fusion = f32[768,1536]{0,1:T(8,128)} fusion(bf16[384,1536]{0,1:T(8,128)(2,1)S(1)} %reshape.32210, bf16[768,384]{1,0:T(8,128)(2,1)S(1)} %bitcast.1145), kind=kOutput, calls=%fused_computation.1 | convolution fusion | flops 905969664 | bytes 6488064 | tf_op jit(solution)/shard_map/dot_general | solution.py:179
  320.6 6.1 %copy.327 = f32[768,1536]{1,0:T(8,128)} copy(f32[768,1536]{0,1:T(8,128)} %convolution_bitcast_fusion) | data formatting | bytes 9437184 | tf_op jit(solution)/shard_map/dot_general | solution.py:179
  326.7 6.6 %reshape.32211 = f32[2,4,2,48,2,2,384]{6,5,4,3,2,1,0:T(2,128)} reshape(f32[768,1536]{1,0:T(8,128)} %copy.327) | data formatting | bytes 9437184 | tf_op jit(solution)/shard_map/reshape | solution.py:184
  333.3 7.2 %fusion.139 = (f32[2,4,1,48,2,1,384]{6,5,4,3,2,1,0:T(1,128)S(1)}, f32[2,4,1,48,2,1,384]{6,5,4,3,2,1,0:T(1,128)S(1)}, f32[2,4,1,48,2,1,384]{6,5,4,3,2,1,0:T(1,128)S(1)}, f32[2,4,1,48,2,1,384]{6,5,4,3,2,1,0:T(1,128)S(1)}) fusion(f32[2,4,2,48,2,2,384]{6,5,4,3,2,1,0:T(2,128)} %reshape.32211), kind=kLoop, calls=%fused_computation.373 | loop fusion | bytes 9437184 | tf_op jit(solution)/shard_map/slice | solution.py:185
  341.1 1.2 copy.332
  (477 shorter events, 30.5 us)
Async XLA Ops:
  6.5 310.4 %copy-start = (bf16[1,2,4,2,48,384]{5,4,3,2,1,0:T(8,128)(2,1)S(1)}, bf16[1,2,4,2,48,384]{5,4,3,2,1,0:T(8,128)(2,1)}, u32[]{:S(2)}) copy-start(bf16[1,2,4,2,48,384]{5,4,3,2,1,0:T(8,128)(2,1)} %param.7) | copy-start | bytes 1769476
  6.6 47.2 %copy-start.20 = (f32[1,3,2,3,3,1,512]{6,5,4,3,2,1,0:T(1,128)S(1)}, f32[1,3,2,3,3,1,512]{6,5,4,3,2,1,0:T(1,128)}, u32[]{:S(2)}) copy-start(f32[1,3,2,3,3,1,512]{6,5,4,3,2,1,0:T(1,128)} %param.6) | copy-start | bytes 331780
  7.7 83.6 %collective-permute-start.2 = (f32[2,3,48,1,512]{4,2,3,1,0:T(8,128)S(1)}, f32[2,3,48,1,512]{4,2,3,1,0:T(8,128)S(1)}, u32[]{:S(2)}, u32[]{:S(2)}) collective-permute-start(f32[2,3,48,1,512]{4,2,3,1,0:T(8,128)S(1)} %bitcast.1146), channel_id=1, source_target_pairs={{0,16},{16,32},{32,48},{48,64},{64,80},{80,96},{96,112},{112,128},... | collective-permute-start | bytes 1769480 | tf_op jit(solution)/shard_map/ppermute | solution.py:27
  13.8 78.0 %collective-permute-start = (f32[2,3,48,1,512]{4,2,3,1,0:T(8,128)S(1)}, f32[2,3,48,1,512]{4,2,3,1,0:T(8,128)S(1)}, u32[]{:S(2)}, u32[]{:S(2)}) collective-permute-start(f32[2,3,48,1,512]{4,2,3,1,0:T(8,128)S(1)} %bitcast.1147), channel_id=1, source_target_pairs={{16,0},{32,16},{48,32},{64,48},{80,64},{96,80},{112,96},{128,112},... | collective-permute-start | bytes 1769480 | tf_op jit(solution)/shard_map/ppermute | solution.py:30
  54.4 36.2 %collective-permute-start.1 = (f32[2,3,3,1,512]{4,3,2,1,0:T(1,128)}, f32[2,3,3,1,512]{4,3,2,1,0:T(1,128)}, u32[]{:S(2)}, u32[]{:S(2)}) collective-permute-start(f32[2,3,3,1,512]{4,3,2,1,0:T(1,128)} %slice_bitcast_fusion.53), channel_id=1, source_target_pairs={{240,0},{0,16},{16,32},{32,48},{48,64},{64,80},{80,96},{96,112},{1... | collective-permute-start | bytes 110600 | tf_op jit(solution)/shard_map/ppermute | solution.py:18
  58.0 8.2 %copy-start.18 = (f32[3,3,1,512]{3,2,1,0:T(1,128)}, f32[3,3,1,512]{3,2,1,0:T(1,128)S(1)}, u32[]{:S(2)}) copy-start(f32[3,3,1,512]{3,2,1,0:T(1,128)S(1)} %get-tuple-element.139) | copy-start | bytes 55300
  58.0 8.2 %copy-start.19 = (f32[3,3,1,512]{3,2,1,0:T(1,128)}, f32[3,3,1,512]{3,2,1,0:T(1,128)S(1)}, u32[]{:S(2)}) copy-start(f32[3,3,1,512]{3,2,1,0:T(1,128)S(1)} %get-tuple-element.140) | copy-start | bytes 55300
  58.0 8.2 %copy-start.21 = (f32[3,3,1,512]{3,2,1,0:T(1,128)}, f32[3,3,1,512]{3,2,1,0:T(1,128)S(1)}, u32[]{:S(2)}) copy-start(f32[3,3,1,512]{3,2,1,0:T(1,128)S(1)} %get-tuple-element.137) | copy-start | bytes 55300
  58.0 8.2 %copy-start.22 = (f32[3,3,1,512]{3,2,1,0:T(1,128)}, f32[3,3,1,512]{3,2,1,0:T(1,128)S(1)}, u32[]{:S(2)}) copy-start(f32[3,3,1,512]{3,2,1,0:T(1,128)S(1)} %get-tuple-element.138) | copy-start | bytes 55300
  70.3 5.4 %copy-start.186 = (s32[8]{0:T(128)}, s32[8]{0:T(128)S(1)}, u32[]{:S(2)}) copy-start(s32[8]{0:T(128)S(1)} %select_reduce_fusion) | copy-start | bytes 100
  74.7 7.8 %copy-start.165 = (f32[1,1,1,512]{3,2,1,0:T(1,128)}, f32[1,1,1,512]{3,2,1,0:T(1,128)S(1)}, u32[]{:S(2)}) copy-start(f32[1,1,1,512]{3,2,1,0:T(1,128)S(1)} %get-tuple-element.149) | copy-start | bytes 6148
  74.7 7.8 %copy-start.167 = (f32[1,1,1,512]{3,2,1,0:T(1,128)}, f32[1,1,1,512]{3,2,1,0:T(1,128)S(1)}, u32[]{:S(2)}) copy-start(f32[1,1,1,512]{3,2,1,0:T(1,128)S(1)} %get-tuple-element.150) | copy-start | bytes 6148
  74.7 7.8 %copy-start.169 = (f32[1,1,1,512]{3,2,1,0:T(1,128)}, f32[1,1,1,512]{3,2,1,0:T(1,128)S(1)}, u32[]{:S(2)}) copy-start(f32[1,1,1,512]{3,2,1,0:T(1,128)S(1)} %get-tuple-element.249) | copy-start | bytes 6148
  74.7 8.5 %copy-start.27 = (f32[1,1,1,512]{3,2,1,0:T(1,128)}, f32[1,1,1,512]{3,2,1,0:T(1,128)S(1)}, u32[]{:S(2)}) copy-start(f32[1,1,1,512]{3,2,1,0:T(1,128)S(1)} %get-tuple-element.144) | copy-start | bytes 6148
  74.7 8.5 %copy-start.29 = (f32[1,1,1,512]{3,2,1,0:T(1,128)}, f32[1,1,1,512]{3,2,1,0:T(1,128)S(1)}, u32[]{:S(2)}) copy-start(f32[1,1,1,512]{3,2,1,0:T(1,128)S(1)} %get-tuple-element.145) | copy-start | bytes 6148
  74.7 8.5 %copy-start.31 = (f32[1,1,1,512]{3,2,1,0:T(1,128)}, f32[1,1,1,512]{3,2,1,0:T(1,128)S(1)}, u32[]{:S(2)}) copy-start(f32[1,1,1,512]{3,2,1,0:T(1,128)S(1)} %get-tuple-element.146) | copy-start | bytes 6148
  74.7 8.5 %copy-start.153 = (f32[1,1,1,512]{3,2,1,0:T(1,128)}, f32[1,1,1,512]{3,2,1,0:T(1,128)S(1)}, u32[]{:S(2)}) copy-start(f32[1,1,1,512]{3,2,1,0:T(1,128)S(1)} %get-tuple-element.143) | copy-start | bytes 6148
  74.7 8.5 %copy-start.155 = (f32[1,1,1,512]{3,2,1,0:T(1,128)}, f32[1,1,1,512]{3,2,1,0:T(1,128)S(1)}, u32[]{:S(2)}) copy-start(f32[1,1,1,512]{3,2,1,0:T(1,128)S(1)} %get-tuple-element.147) | copy-start | bytes 6148
  74.7 8.5 %copy-start.157 = (f32[1,1,1,512]{3,2,1,0:T(1,128)}, f32[1,1,1,512]{3,2,1,0:T(1,128)S(1)}, u32[]{:S(2)}) copy-start(f32[1,1,1,512]{3,2,1,0:T(1,128)S(1)} %get-tuple-element.148) | copy-start | bytes 6148
  75.6 6.8 %copy-start.171 = (f32[1,1,1,512]{3,2,1,0:T(1,128)}, f32[1,1,1,512]{3,2,1,0:T(1,128)S(1)}, u32[]{:S(2)}) copy-start(f32[1,1,1,512]{3,2,1,0:T(1,128)S(1)} %get-tuple-element.152) | copy-start | bytes 6148
  75.6 6.8 %copy-start.173 = (f32[1,1,1,512]{3,2,1,0:T(1,128)}, f32[1,1,1,512]{3,2,1,0:T(1,128)S(1)}, u32[]{:S(2)}) copy-start(f32[1,1,1,512]{3,2,1,0:T(1,128)S(1)} %get-tuple-element.158) | copy-start | bytes 6148
  75.6 6.8 %copy-start.175 = (f32[1,1,1,512]{3,2,1,0:T(1,128)}, f32[1,1,1,512]{3,2,1,0:T(1,128)S(1)}, u32[]{:S(2)}) copy-start(f32[1,1,1,512]{3,2,1,0:T(1,128)S(1)} %get-tuple-element.250) | copy-start | bytes 6148
  75.6 7.6 %copy-start.33 = (f32[1,1,1,512]{3,2,1,0:T(1,128)}, f32[1,1,1,512]{3,2,1,0:T(1,128)S(1)}, u32[]{:S(2)}) copy-start(f32[1,1,1,512]{3,2,1,0:T(1,128)S(1)} %get-tuple-element.155) | copy-start | bytes 6148
  75.6 7.6 %copy-start.35 = (f32[1,1,1,512]{3,2,1,0:T(1,128)}, f32[1,1,1,512]{3,2,1,0:T(1,128)S(1)}, u32[]{:S(2)}) copy-start(f32[1,1,1,512]{3,2,1,0:T(1,128)S(1)} %get-tuple-element.156) | copy-start | bytes 6148
  75.7 7.6 %copy-start.37 = (f32[1,1,1,512]{3,2,1,0:T(1,128)}, f32[1,1,1,512]{3,2,1,0:T(1,128)S(1)}, u32[]{:S(2)}) copy-start(f32[1,1,1,512]{3,2,1,0:T(1,128)S(1)} %get-tuple-element.157) | copy-start | bytes 6148
  75.7 7.6 %copy-start.159 = (f32[1,1,1,512]{3,2,1,0:T(1,128)}, f32[1,1,1,512]{3,2,1,0:T(1,128)S(1)}, u32[]{:S(2)}) copy-start(f32[1,1,1,512]{3,2,1,0:T(1,128)S(1)} %get-tuple-element.151) | copy-start | bytes 6148
  75.7 7.6 %copy-start.161 = (f32[1,1,1,512]{3,2,1,0:T(1,128)}, f32[1,1,1,512]{3,2,1,0:T(1,128)S(1)}, u32[]{:S(2)}) copy-start(f32[1,1,1,512]{3,2,1,0:T(1,128)S(1)} %get-tuple-element.153) | copy-start | bytes 6148
  75.7 7.6 %copy-start.163 = (f32[1,1,1,512]{3,2,1,0:T(1,128)}, f32[1,1,1,512]{3,2,1,0:T(1,128)S(1)}, u32[]{:S(2)}) copy-start(f32[1,1,1,512]{3,2,1,0:T(1,128)S(1)} %get-tuple-element.154) | copy-start | bytes 6148
  76.8 3.8 %copy-start.129 = (f32[1,1,1,512]{3,2,1,0:T(1,128)}, f32[1,1,1,512]{3,2,1,0:T(1,128)S(1)}, u32[]{:S(2)}) copy-start(f32[1,1,1,512]{3,2,1,0:T(1,128)S(1)} %get-tuple-element.226) | copy-start | bytes 6148
  76.9 4.5 %copy-start.117 = (f32[1,1,1,512]{3,2,1,0:T(1,128)}, f32[1,1,1,512]{3,2,1,0:T(1,128)S(1)}, u32[]{:S(2)}) copy-start(f32[1,1,1,512]{3,2,1,0:T(1,128)S(1)} %get-tuple-element.222) | copy-start | bytes 6148
  76.9 4.5 %copy-start.119 = (f32[1,1,1,512]{3,2,1,0:T(1,128)}, f32[1,1,1,512]{3,2,1,0:T(1,128)S(1)}, u32[]{:S(2)}) copy-start(f32[1,1,1,512]{3,2,1,0:T(1,128)S(1)} %get-tuple-element.229) | copy-start | bytes 6148
  76.9 4.5 %copy-start.121 = (f32[1,1,1,512]{3,2,1,0:T(1,128)}, f32[1,1,1,512]{3,2,1,0:T(1,128)S(1)}, u32[]{:S(2)}) copy-start(f32[1,1,1,512]{3,2,1,0:T(1,128)S(1)} %get-tuple-element.230) | copy-start | bytes 6148
  76.9 4.5 %copy-start.123 = (f32[1,1,1,512]{3,2,1,0:T(1,128)}, f32[1,1,1,512]{3,2,1,0:T(1,128)S(1)}, u32[]{:S(2)}) copy-start(f32[1,1,1,512]{3,2,1,0:T(1,128)S(1)} %get-tuple-element.282) | copy-start | bytes 6148
  76.9 4.5 %copy-start.125 = (f32[1,1,1,512]{3,2,1,0:T(1,128)}, f32[1,1,1,512]{3,2,1,0:T(1,128)S(1)}, u32[]{:S(2)}) copy-start(f32[1,1,1,512]{3,2,1,0:T(1,128)S(1)} %get-tuple-element.283) | copy-start | bytes 6148
  76.9 4.5 %copy-start.127 = (f32[1,1,1,512]{3,2,1,0:T(1,128)}, f32[1,1,1,512]{3,2,1,0:T(1,128)S(1)}, u32[]{:S(2)}) copy-start(f32[1,1,1,512]{3,2,1,0:T(1,128)S(1)} %get-tuple-element.290) | copy-start | bytes 6148
  94.5 17.2 %collective-permute-start.3 = (f32[2,3,48,1,512]{4,2,1,3,0:T(8,128)S(1)}, f32[2,3,48,1,512]{4,2,1,3,0:T(8,128)S(1)}, u32[]{:S(2)}, u32[]{:S(2)}) collective-permute-start(f32[2,3,48,1,512]{4,2,1,3,0:T(8,128)S(1)} %get-tuple-element.111), channel_id=1, source_target_pairs={{16,0},{32,16},{48,32},{64,48},{80,64},{96,80},{112,96},{128,112},... | collective-permute-start | bytes 1769480 | tf_op jit(solution)/shard_map/ppermute | solution.py:30
  99.6 17.4 %collective-permute-start.4 = (f32[2,3,48,1,512]{4,2,1,3,0:T(8,128)S(1)}, f32[2,3,48,1,512]{4,2,1,3,0:T(8,128)S(1)}, u32[]{:S(2)}, u32[]{:S(2)}) collective-permute-start(f32[2,3,48,1,512]{4,2,1,3,0:T(8,128)S(1)} %get-tuple-element.111), channel_id=1, source_target_pairs={{0,16},{16,32},{32,48},{48,64},{64,80},{80,96},{96,112},{112,128},... | collective-permute-start | bytes 1769480 | tf_op jit(solution)/shard_map/ppermute | solution.py:27
  119.4 9.3 %copy-start.181 = (s32[2]{0:T(128)S(1)}, s32[2]{0:T(128)}, u32[]{:S(2)}) copy-start(s32[2]{0:T(128)} %get-tuple-element.5) | copy-start | bytes 28
  119.4 9.3 %copy-start.182 = (s32[2]{0:T(128)S(1)}, s32[2]{0:T(128)}, u32[]{:S(2)}) copy-start(s32[2]{0:T(128)} %get-tuple-element.6) | copy-start | bytes 28
  119.4 9.3 %copy-start.183 = (f32[2]{0:T(128)S(1)}, f32[2]{0:T(128)}, u32[]{:S(2)}) copy-start(f32[2]{0:T(128)} %multiply_reduce_fusion) | copy-start | bytes 28
  119.5 9.3 %copy-start.184 = (s32[64]{0:T(128)S(1)}, s32[64]{0:T(128)}, u32[]{:S(2)}) copy-start(s32[64]{0:T(128)} %get-tuple-element.300) | copy-start | bytes 772
  119.5 9.3 %copy-start.185 = (s32[64]{0:T(128)S(1)}, s32[64]{0:T(128)}, u32[]{:S(2)}) copy-start(s32[64]{0:T(128)} %get-tuple-element.301) | copy-start | bytes 772
  119.5 9.5 %copy-start.187 = (s32[8]{0:T(128)S(1)}, s32[8]{0:T(128)}, u32[]{:S(2)}) copy-start(s32[8]{0:T(128)} %copy-done.186) | copy-start | bytes 100
  121.4 18.3 %all-to-all-start = ((bf16[8,2,9216]{2,1,0:T(2,128)(2,1)}), bf16[8,2,9216]{2,1,0:T(2,128)(2,1)S(1)}, u32[]{:S(2)}, u32[]{:S(2)}) async-start(bf16[8,2,9216]{2,1,0:T(2,128)(2,1)} %reshape.32232), calls=%async_computation | async-start | bytes 589824 | tf_op jit(solution)/shard_map/all_to_all | solution.py:152
  128.7 81.4 %reduce-scatter.4.cloned.1.call-start = ((), (), s32[]{:S(2)}) async-start(), calls=%async_computation.2 | async-start | bytes 2506752 | tf_op jit(solution)/shard_map/reduce_scatter | solution.py:38
  147.4 163.8 %all-gather.3.cloned.1.call-start = ((), (), s32[]{:S(2)}) async-start(), calls=%async_computation.3 | async-start | bytes 1327104 | tf_op jit(solution)/shard_map/all_gather | solution.py:51
  230.3 7.3 %collective-permute-start.5 = (bf16[384,16]{0,1:T(8,128)(2,1)S(1)}, bf16[384,16]{0,1:T(8,128)(2,1)S(1)}, u32[]{:S(2)}, u32[]{:S(2)}) collective-permute-start(bf16[384,16]{0,1:T(8,128)(2,1)S(1)} %convert.27), channel_id=1, source_target_pairs={{0,2},{2,4},{4,6},{6,8},{8,10},{10,12},{12,14},{1,3},{3,5},{5,7},{... | collective-permute-start | bytes 36872
  232.7 4.9 %collective-permute-start.6 = (bf16[384,12]{0,1:T(8,128)(2,1)S(1)}, bf16[384,12]{0,1:T(8,128)(2,1)S(1)}, u32[]{:S(2)}, u32[]{:S(2)}) collective-permute-start(bf16[384,12]{0,1:T(8,128)(2,1)S(1)} %slice.1885), channel_id=1, source_target_pairs={{0,4},{2,6},{4,8},{6,10},{8,12},{10,14},{1,5},{3,7},{5,9},{7,11},{... | collective-permute-start | bytes 27656
  (150 other events, 178.1 us)
Sparse Core Ops, SparseCore 0:
  147.5 62.5 reduce-scatter.3
  267.3 43.8 all-gather.2
where the time goes:
time: 352 us; the launch traced here: 349 us
  waiting for transfers between devices  127 us (36%)
  starting transfers between devices  68 us (19%)
  local copies, waits for them, and re-layouts  64.4 us (18%)
  blocking collectives  48.6 us (14%)
  other arithmetic  19.9 us (6%)
  between operations  16.7 us (5%)
  matrix products  4.46 us (1%)
    reduce_scatter x1, waiting for transfers between devices, scatter_axes(): nearer = lax.psum_scatter(shard, axes[0], scatter_dimension=dim, tiled=True)  62.6 us
    ppermute x2, starting transfers between devices, with_halo(): lax.ppermute(lax.slice_in_dim(block, 0, width, axis=dim), axis, backward)  45.1 us
    all_gather x1, waiting for transfers between devices, gather_in_order(): blocks = lax.all_gather(blocks, axes[k], axis=0, tiled=True)  44.1 us
    all_gather x1, blocking collectives, gather_in_order(): blocks = lax.all_gather(blocks, axes[k], axis=0, tiled=True)  28.3 us
    unnamed x1, blocking collectives  20.2 us
    unnamed x383, local copies, waits for them, and re-layouts  11.3 us
    all_to_all x1, waiting for transfers between devices, per_device(): lax.all_to_all(filtered, 'vec', split_axis=4, concat_axis=2, tiled=True)  10.6 us
    another operation x36, other arithmetic, link_times(): return (jnp.stack(result_re), jnp.stack(result_im))  8.82 us
  transfers between devices with their start and end apart: 10, of which 5 were waited for; matrix products, arithmetic and copies ran while one was open for 11% of the time, Pallas kernels for 0%

commit v1 on v0

v1 whole, which is shorter than its diff:
```python
import functools
import math

import jax
import jax.numpy as jnp
from jax import lax
from jax.experimental import pallas as pl
from jax.experimental.pallas import tpu as pltpu
from jax.sharding import PartitionSpec as P

LX = 32
LY = 16
LANES = 128
ROWS = 16
MESH = pl.DeviceIdType.MESH
F32 = jnp.float32
BF16 = jnp.bfloat16

two_pi = 2.0 * math.pi

ORDER = (
    "f0 f1 F01 f2",
    "F02 F11 F03 F12",
    "F04 M0 F21 F13",
    "F22 F14 M1 F23",
    "R0 F24 M2 R1",
    "Z0 R2 X01 Z1",
    "X02 X11 Z2 X03",
    "X12 X21 X04 X13",
    "X22 X14 X23 X24",
)


def link_times(entry, re, im, dagger):
    out_re, out_im = [], []
    for target in range(3):
        total_re = total_im = None
        for source in range(3):
            place = source * 3 + target if dagger else target * 3 + source
            ere, eim = entry[place], entry[9 + place]
            if dagger:
                tre = ere * re[source] + eim * im[source]
                tim = ere * im[source] - eim * re[source]
            else:
                tre = ere * re[source] - eim * im[source]
                tim = ere * im[source] + eim * re[source]
            total_re = tre if total_re is None else total_re + tre
            total_im = tim if total_im is None else total_im + tim
        out_re.append(total_re)
        out_im.append(total_im)
    return out_re + out_im


def elementals(
    ring, sites, chunks, momenta_count,
    x0, links, owner, momenta, phi_out,
    shifted_links, lk, cs, t1, acc, raw0, back0, raw1, back1, above0, below0, above1, below1,
    weights, *rest,
):
    gathered, parts, rs_in, phi = (rest[k * chunks : (k + 1) * chunks] for k in range(4))
    halo_send, halo_recv, f_send, f_recv, rs_send, rs_recv, z_send, z_recv, x_send, x_recv = rest[4 * chunks :]
    x = lax.axis_index("vec")
    z = lax.axis_index("site")
    plane = links.shape[-1]
    tiles = plane // LANES
    block = chunks * ROWS
    half_ring = ring // 2
    groups = parts[0].shape[0]
    group_rows = parts[0].shape[1]

    barrier = pltpu.get_barrier_semaphore()

    def greet(d, carry):
        pl.semaphore_signal(barrier, inc=1, device_id={"site": lax.rem(z + d, sites)}, device_id_type=MESH)
        return carry

    lax.fori_loop(1, sites, greet, 0)
    for d in (1, ring - 1):
        pl.semaphore_signal(barrier, inc=1, device_id={"vec": lax.rem(x + d, ring)}, device_id_type=MESH)

    column = lax.broadcasted_iota(jnp.int32, (18, plane), 1) % LX
    link_x, link_y = links[0:18], links[18:36]
    shifted_links[0:18] = link_x
    shifted_links[18:36] = jnp.where(
        column == 0, pltpu.roll(link_x, plane + 1 - LX, 1), pltpu.roll(link_x, 1, 1)
    )
    shifted_links[36:54] = link_y
    shifted_links[54:72] = pltpu.roll(link_y, LX, 1)
    shifted_links[72:90] = links[36:54]

    def spread(e, carry):
        lk[e] = jnp.broadcast_to(shifted_links[pl.ds(e, 1), :], (8, plane))
        return carry

    lax.fori_loop(0, 90, spread, 0)

    flat = lax.broadcasted_iota(jnp.int32, (8, plane), 1)
    for p in range(momenta_count):
        theta = two_pi * (
            (momenta[p, 0] * (flat % LX)).astype(F32) / LX
            + (momenta[p, 1] * (flat // LX)).astype(F32) / LY
            + (jnp.zeros_like(flat) + momenta[p, 2] * z).astype(F32) / sites
        )
        cs[p, 0] = jnp.cos(theta)
        cs[p, 1] = jnp.sin(theta)

    def lanes_of(t):
        return pl.ds(pl.multiple_of(t * LANES, LANES), LANES)

    def entries(hop, lanes):
        return [lk[hop * 18 + e, :, lanes][None] for e in range(18)]

    def vectors(ref, c, lanes):
        return [ref[comp, pl.ds(2 * c, 2), :, lanes] for comp in range(6)]

    def pack(value):
        return value.reshape(ROWS, LANES).astype(BF16)

    def unpack(value):
        return value.astype(F32).reshape(2, 8, LANES)

    lane = lax.broadcasted_iota(jnp.int32, (2, 8, LANES), 2)
    last_column = lane % LX == LX - 1
    first_column = lane % LX == 0

    def roll(value, shift):
        return pltpu.roll(value.reshape(ROWS, LANES), shift, 1).reshape(2, 8, LANES)

    def outgoing(source, raw, back, c):
        def body(t, carry):
            lanes = lanes_of(t)
            field = vectors(source, c, lanes)
            sent = link_times(entries(4, lanes), field[:3], field[3:], True)
            for comp in range(6):
                raw[c, comp, :, lanes] = pack(field[comp])
                back[c, comp, :, lanes] = pack(sent[comp])
            return carry

        lax.fori_loop(0, tiles, body, 0)

    def in_plane(source, c):
        def body(t, carry):
            lanes = lanes_of(t)
            field = vectors(source, c, lanes)
            ahead = [jnp.where(last_column, roll(w, LX - 1), roll(w, LANES - 1)) for w in field]
            total = link_times(entries(0, lanes), ahead[:3], ahead[3:], False)
            behind = [jnp.where(first_column, roll(w, LANES + 1 - LX), roll(w, 1)) for w in field]
            added = link_times(entries(1, lanes), behind[:3], behind[3:], True)
            total = [a + b for a, b in zip(total, added)]
            after = vectors(source, c, lanes_of(lax.rem(t + 1, tiles)))
            ahead = [
                jnp.where(lane < LANES - LX, roll(w, LANES - LX), roll(v, LANES - LX)) for w, v in zip(field, after)
            ]
            added = link_times(entries(2, lanes), ahead[:3], ahead[3:], False)
            total = [a + b for a, b in zip(total, added)]
            before = vectors(source, c, lanes_of(lax.rem(t + tiles - 1, tiles)))
            behind = [jnp.where(lane >= LX, roll(w, LX), roll(v, LX)) for w, v in zip(field, before)]
            added = link_times(entries(3, lanes), behind[:3], behind[3:], True)
            for comp in range(6):
                acc[comp, pl.ds(2 * c, 2), :, lanes] = total[comp] + added[comp]
            return carry

        lax.fori_loop(0, tiles, body, 0)

    def applied(c, lanes, above, below):
        total = vectors(acc, c, lanes)
        field = [unpack(above[c, comp, :, lanes]) for comp in range(6)]
        added = link_times(entries(4, lanes), field[:3], field[3:], False)
        return [
            (total[comp] + added[comp] + unpack(below[c, comp, :, lanes])) * (-1.0 / 6.0) for comp in range(6)
        ]

    up, down = lax.rem(z + 1, sites), lax.rem(z + sites - 1, sites)
    started = []

    def halo(round_, c):
        raw, back, above, below = (raw0, back0, above0, below0) if round_ == 0 else (raw1, back1, above1, below1)
        return [
            pltpu.make_async_remote_copy(
                src_ref=raw.at[c], dst_ref=above.at[c],
                send_sem=halo_send.at[round_, 0, c], recv_sem=halo_recv.at[round_, 0, c],
                device_id={"site": down}, device_id_type=MESH,
            ),
            pltpu.make_async_remote_copy(
                src_ref=back.at[c], dst_ref=below.at[c],
                send_sem=halo_send.at[round_, 1, c], recv_sem=halo_recv.at[round_, 1, c],
                device_id={"site": up}, device_id_type=MESH,
            ),
        ]

    def send_halo(round_, c):
        for copy in halo(round_, c):
            copy.start()
            started.append(copy)

    def wait_halo(round_, c):
        for copy in halo(round_, c):
            copy.wait_recv()

    for c in range(chunks):
        outgoing(x0, raw0, back0, c)
    pl.semaphore_wait(barrier, sites - 1 + 2)
    for c in range(chunks):
        send_halo(0, c)
    for c in range(chunks):
        in_plane(x0, c)
    for c in range(chunks):
        wait_halo(0, c)

        def first(t, carry, c=c):
            lanes = lanes_of(t)
            result = applied(c, lanes, above0, below0)
            sent = link_times(entries(4, lanes), result[:3], result[3:], True)
            for comp in range(6):
                t1[comp, pl.ds(2 * c, 2), :, lanes] = result[comp]
                raw1[c, comp, :, lanes] = pack(result[comp])
                back1[c, comp, :, lanes] = pack(sent[comp])
            return carry

        lax.fori_loop(0, tiles, first, 0)
        send_halo(1, c)
        in_plane(t1, c)

    def ring_copy(buffers, span, sends, recvs, way, c, step, half, block_of):
        sign = 1 if way == 0 else ring - 1
        here = buffers[c].at[block_of, pl.ds(half * span, span)]
        return pltpu.make_async_remote_copy(
            src_ref=here, dst_ref=here,
            send_sem=sends.at[way, c, step - 1, half], recv_sem=recvs.at[way, c, step - 1, half],
            device_id={"vec": lax.rem(x + sign, ring)}, device_id_type=MESH,
        )

    def ring_send(buffers, span, sends, recvs, c, step, half, way):
        if step == half_ring and half != way:
            return
        back_by = (ring - (step - 1)) if way == 0 else (step - 1)
        copy = ring_copy(buffers, span, sends, recvs, way, c, step, half, lax.rem(x + back_by, ring))
        copy.start()
        started.append(copy)

    def ring_forward(buffers, span, sends, recvs, c, step):
        for half in range(2):
            for way in range(2):
                if step == half_ring and half != way:
                    continue
                back_by = (ring - step) if way == 0 else step
                ring_copy(
                    buffers, span, sends, recvs, way, c, step, half, lax.rem(x + back_by, ring)
                ).wait_recv()
                if step < half_ring:
                    ring_send(buffers, span, sends, recvs, c, step + 1, half, way)

    vectors_ring = (gathered, 3, f_send, f_recv)
    elemental_rows = phi[0].shape[1] // 2
    phi_ring = (phi, elemental_rows, x_send, x_recv)

    def start_ring(which, c):
        for half in range(2):
            for way in range(2):
                ring_send(*which, c, 1, half, way)

    def filter_chunk(c):
        wait_halo(1, c)

        def second(t, carry):
            lanes = lanes_of(t)
            result = applied(c, lanes, above1, below1)
            start = vectors(x0, c, lanes)
            for comp in range(6):
                gathered[c][x, comp, :, lanes] = pack(2.0 * result[comp] - start[comp])
            return carry

        lax.fori_loop(0, tiles, second, 0)
        start_ring(vectors_ring, c)

        def phases(t, carry):
            lanes = lanes_of(t)
            for color in range(3):
                re = unpack(gathered[c][x, color, :, lanes])
                im = unpack(gathered[c][x, 3 + color, :, lanes])
                for p in range(momenta_count):
                    cosine, sine = cs[p, 0, :, lanes][None], cs[p, 1, :, lanes][None]
                    shift_re = pack(cosine * re + sine * im)
                    shift_im = pack(cosine * im - sine * re)
                    real = pl.ds(2 * p * block + c * ROWS, ROWS)
                    imag = pl.ds((2 * p + 1) * block + c * ROWS, ROWS)
                    weights[color, real, lanes] = shift_re
                    weights[3 + color, real, lanes] = shift_im
                    weights[color, imag, lanes] = shift_im
                    weights[3 + color, imag, lanes] = -shift_re
            return carry

        lax.fori_loop(0, tiles, phases, 0)

    inverse = []
    for place in range(ring):
        found = 0
        for b in range(ring):
            found = jnp.where(owner[b] == place, b, found)
        inverse.append(found)

    def group_of(device):
        index = (device * groups + sites - 1) // sites
        return index, jnp.logical_and(index < groups, (index * sites) // groups == device)

    my_group, reduces = group_of(z)
    spare = jnp.where(reduces, my_group, 0)

    def far_first(i):
        k = (i + 1) // 2
        return sites // 2 + jnp.where(i % 2 == 0, k, -k)

    def partial_copy(c, group, target, source):
        return pltpu.make_async_remote_copy(
            src_ref=parts[c].at[group], dst_ref=rs_in[c].at[source],
            send_sem=rs_send.at[c, group], recv_sem=rs_recv.at[c, source],
            device_id={"site": target}, device_id_type=MESH,
        )

    def multiply(c):
        total = None
        for comp in range(6):
            left = weights[comp]
            right = jnp.concatenate([gathered[c][inverse[place], comp] for place in range(ring)], axis=0)
            product = lax.dot_general(left, right, (((1,), (1,)), ((), ())), preferred_element_type=F32)
            total = product if total is None else total + product
        parts[c][...] = total.reshape(groups, group_rows, ring * ROWS).astype(BF16)

        def send(i, carry):
            target = lax.rem(z + far_first(i), sites)
            group, valid = group_of(target)

            @pl.when(valid)
            def _():
                partial_copy(c, group, target, z).start()

            return carry

        lax.fori_loop(0, sites - 1, send, 0)

    def z_copy(c, group, target, number):
        rows = pl.ds(pl.multiple_of(group * group_rows, ROWS), group_rows)
        here = phi[c].at[x, rows]
        return pltpu.make_async_remote_copy(
            src_ref=here, dst_ref=here,
            send_sem=z_send.at[c, number], recv_sem=z_recv.at[c, group],
            device_id={"site": target}, device_id_type=MESH,
        )

    def reduce(c):
        @pl.when(reduces)
        def _():
            def arrive(i, carry):
                source = lax.rem(z + i, sites)
                partial_copy(c, spare, z, source).wait_recv()
                return carry

            lax.fori_loop(1, sites, arrive, 0)

            def add(i, total):
                return total + rs_in[c][lax.rem(z + i, sites)].astype(F32)

            total = lax.fori_loop(1, sites, add, parts[c][spare].astype(F32))
            rows = pl.ds(pl.multiple_of(spare * group_rows, ROWS), group_rows)
            phi[c][x, rows, :] = total.astype(BF16)

            def send(i, carry):
                z_copy(c, spare, lax.rem(z + far_first(i), sites), i).start()
                return carry

            lax.fori_loop(0, sites - 1, send, 0)

    def gather_planes(c):
        def arrive(i, carry):
            device = lax.rem(z + i, sites)
            group, valid = group_of(device)

            @pl.when(valid)
            def _():
                z_copy(c, group, device, 0).wait_recv()

            return carry

        lax.fori_loop(1, sites, arrive, 0)
        start_ring(phi_ring, c)

    for op in " ".join(ORDER).split():
        c, step = int(op[1]), int(op[2:] or 0)
        if step > half_ring:
            continue
        if op[0] == "f":
            filter_chunk(c)
        elif op[0] == "F":
            ring_forward(*vectors_ring, c, step)
        elif op[0] == "M":
            multiply(c)
        elif op[0] == "R":
            reduce(c)
        elif op[0] == "Z":
            gather_planes(c)
        else:
            ring_forward(*phi_ring, c, step)
    for c in range(chunks):
        phi_out[c] = phi[c][...]

    for copy in started:
        copy.wait_send()
    for c in range(chunks):

        def sent(i, carry, c=c):
            group, valid = group_of(lax.rem(z + i, sites))

            @pl.when(valid)
            def _():
                partial_copy(c, group, z, z).wait_send()

            return carry

        lax.fori_loop(1, sites, sent, 0)

        @pl.when(reduces)
        def _(c=c):
            def gone(i, carry):
                z_copy(c, spare, z, i).wait_send()
                return carry

            lax.fori_loop(0, sites - 1, gone, 0)


def project(ring, chunks, momenta_count, phi, tau, owner, out, ordered, turned):
    block = chunks * ROWS
    width = ring * block
    piece = ring * ROWS
    for place in range(ring):
        source = 0
        for b in range(ring):
            source = jnp.where(owner[b] == place, b, source)
        for c in range(chunks):
            ordered[:, place * block : (place + 1) * block, c * piece : (c + 1) * piece] = phi[c, source].reshape(
                2 * momenta_count, block, piece
            )
    row = lax.broadcasted_iota(jnp.int32, (width, width), 0)
    spot = lax.broadcasted_iota(jnp.int32, (width, width), 1)
    origin = ((spot % piece) // ROWS) * block + (spot // piece) * ROWS + spot % ROWS
    swap = jnp.where(row == origin, 1.0, 0.0).astype(BF16)
    outer = tau.shape[0]
    for part in range(2):
        rows = tau[:, part].reshape(outer * block, width)
        turned[part] = jnp.dot(rows, swap, preferred_element_type=F32).astype(BF16)
    turned[2] = -turned[1]

    def times(a, p, b):
        return lax.dot_general(turned[a], ordered[2 * p + b], (((1,), (1,)), ((), ())), preferred_element_type=F32)

    for p in range(momenta_count):
        real = times(0, p, 0) + times(2, p, 1)
        out[:, p, 0] = real.astype(BF16).reshape(outer, block, width)
        imag = times(0, p, 1) + times(1, p, 0)
        out[:, p, 1] = imag.astype(BF16).reshape(outer, block, width)


def per_device(eigvecs, links, peramb, block_owner, momenta):
    ring, sites = lax.axis_size("vec"), lax.axis_size("site")
    block = eigvecs.shape[3]
    plane = eigvecs.shape[5]
    chunks = block // ROWS
    momenta_count = momenta.shape[0]
    rows = 2 * momenta_count * block
    groups = max(g for g in range(1, sites + 1) if (rows // ROWS) % g == 0)
    group_rows = rows // groups
    piece = ring * ROWS
    half_ring = ring // 2
    x0 = eigvecs.reshape(6, block // 8, 8, plane)
    table = links.reshape(54, plane)
    vmem = pl.BlockSpec(memory_space=pltpu.VMEM)
    smem = pl.BlockSpec(memory_space=pltpu.SMEM)
    packed = pltpu.VMEM((chunks, 6, ROWS, plane), BF16)
    field = pltpu.VMEM((6, block // 8, 8, plane), F32)
    dma = pltpu.SemaphoreType.DMA
    phi = pl.pallas_call(
        functools.partial(elementals, ring, sites, chunks, momenta_count),
        out_shape=jax.ShapeDtypeStruct((chunks, ring, rows, piece), BF16),
        in_specs=[vmem, vmem, smem, smem],
        out_specs=vmem,
        scratch_shapes=[
            pltpu.VMEM((90, plane), F32),
            pltpu.VMEM((90, 8, plane), F32),
            pltpu.VMEM((momenta_count, 2, 8, plane), F32),
            field,
            field,
            *[packed] * 8,
            pltpu.VMEM((6, rows, plane), BF16),
            *[pltpu.VMEM((ring, 6, ROWS, plane), BF16)] * chunks,
            *[pltpu.VMEM((groups, group_rows, piece), BF16)] * chunks,
            *[pltpu.VMEM((sites, group_rows, piece), BF16)] * chunks,
            *[pltpu.VMEM((ring, rows, piece), BF16)] * chunks,
            dma((2, 2, chunks)),
            dma((2, 2, chunks)),
            dma((2, chunks, half_ring, 2)),
            dma((2, chunks, half_ring, 2)),
            dma((chunks, groups)),
            dma((chunks, sites)),
            dma((chunks, sites)),
            dma((chunks, groups)),
            dma((2, chunks, half_ring, 2)),
            dma((2, chunks, half_ring, 2)),
        ],
        compiler_params=pltpu.CompilerParams(collective_id=0, has_side_effects=True),
        name="elementals",
    )(x0, table, block_owner, momenta)
    sinks, spins = peramb.shape[1], peramb.shape[2]
    width = ring * block
    tau = peramb.reshape(sinks * spins, 2, block, width)
    result = pl.pallas_call(
        functools.partial(project, ring, chunks, momenta_count),
        out_shape=jax.ShapeDtypeStruct((sinks * spins, momenta_count, 2, block, width), BF16),
        in_specs=[vmem, vmem, smem],
        out_specs=vmem,
        scratch_shapes=[
            pltpu.VMEM((2 * momenta_count, width, width), BF16),
            pltpu.VMEM((3, sinks * spins * block, width), BF16),
        ],
        name="project",
    )(phi, tau, block_owner)
    return result.reshape(1, sinks, spins, momenta_count, 2, block, width)


def solution(mesh):
    placed = (
        P(("cfg", "tslice"), None, None, "vec", "site", None),
        P(("cfg", "tslice"), None, None, None, None, "site", None),
        P(("cfg", "tslice"), "site", None, None, "vec", None),
        P(),
        P(),
    )
    return jax.shard_map(
        per_device,
        mesh=mesh,
        in_specs=placed,
        out_specs=P(("cfg", "tslice"), "site", None, None, None, "vec", None),
        check_vma=False,
    )
```

time: 352 us -> 133 us (0.38)
  Pallas kernels: 0 us -> 129 us
  waiting for transfers between devices: 127 us -> 0 us
  starting transfers between devices: 68 us -> 0 us
  local copies, waits for them, and re-layouts: 64.4 us -> 2.64 us
  blocking collectives: 48.6 us -> 0 us
  other arithmetic: 19.9 us -> 1.19 us
  between operations: 16.7 us -> 0.01 us
  matrix products: 4.46 us -> 0 us
    pallas_call x0 -> x2, Pallas kernels: none -> 129 us  [the longest x1 125 us: per_device(): pl.pallas_call(functools.partial(elementals, ring, sites, chunks, momenta...]
    reduce_scatter x1 -> x0, waiting for transfers between devices: 62.6 us -> none  [scatter_axes(): nearer = lax.psum_scatter(shard, axes[0], scatter_dimension=dim, tiled=True)]
    ppermute x5 -> x0, starting transfers between devices: 55.2 us -> none  [the longest x2 45.1 us: with_halo(): lax.ppermute(lax.slice_in_dim(block, 0, width, axis=dim), axis, backward)]
    all_gather x1 -> x0, waiting for transfers between devices: 44.1 us -> none  [gather_in_order(): blocks = lax.all_gather(blocks, axes[k], axis=0, tiled=True)]
    all_gather x1 -> x0, blocking collectives: 28.3 us -> none  [gather_in_order(): blocks = lax.all_gather(blocks, axes[k], axis=0, tiled=True)]
    slice x26 -> x0, local copies, waits for them, and re-layouts: 22.7 us -> none  [the longest x1 7.22 us: per_device(): real_part = layout[:, :, 0, :, :, 0] - layout[:, :, 1, :, :, 1]]
    unnamed x1 -> x0, blocking collectives: 20.2 us -> none
    all_to_all x1 -> x0, waiting for transfers between devices: 10.6 us -> none  [per_device(): lax.all_to_all(filtered, 'vec', split_axis=4, concat_axis=2, tiled=True)]
  transfers between devices with their start and end apart: 10 -> 0, of which waited for: 5 -> 0; matrix products, arithmetic and copies ran while one was open for 11% -> 0% of each run, Pallas kernels for 0% -> 0%
where the time goes in v1:
time: 133 us
  Pallas kernels  129 us (97%)
  local copies, waits for them, and re-layouts  2.64 us (2%)
    pallas_call x1, Pallas kernels, per_device(): pl.pallas_call(functools.partial(elementals, ring, sites, chunks, momenta...  125 us
    pallas_call x1, Pallas kernels, per_device(): pl.pallas_call(functools.partial(project, ring, chunks, momenta_count), o...  4.52 us

profile of v1, /device:TPU:80, one launch (start us, length us, event | category | flops | bytes accessed | tf_op | source)
XLA Modules:
  0.0 133.2 jit_solution(4084659893773291501)
XLA Ops:
  0.0 1.2 reduce
  1.2 0.7 reshape.13.links
  1.9 1.9 %copy.6 = f32[1,2,3,48,1,512]{5,3,4,2,1,0:T(8,128)} copy(f32[1,2,3,48,1,512]{5,4,3,2,1,0:T(1,128)} %param.5) | data formatting | bytes 1179648
  3.8 124.9 %elementals.1.phi = bf16[3,8,192,128]{3,2,1,0:T(8,128)(2,1)} custom-call(f32[6,6,8,512]{3,2,1,0:T(8,128)} %bitcast.3, f32[54,512]{1,0:T(8,128)} %reshape.13.links, s32[8]{0:T(128)} %owner.3, s32[2,3]{1,0:T(2,128)} %momenta.1), custom_call_target="tpu_custom_call" | custom-call | tf_op jit(solution)/shard_map/elementals/pallas_call | solution.py:480
  128.7 4.5 %project.1 = bf16[8,2,2,48,384]{4,3,2,1,0:T(8,128)(2,1)} custom-call(bf16[3,8,192,128]{3,2,1,0:T(8,128)(2,1)} %elementals.1.phi, bf16[8,2,48,384]{3,2,1,0:T(8,128)(2,1)} %bitcast.4, s32[8]{0:T(128)} %owner.3), custom_call_target="tpu_custom_call" | custom-call | tf_op jit(solution)/shard_map/project/pallas_call | solution.py:514

commit v2 on v1

v2 whole, which is shorter than its diff:
```python
import functools
import math

import jax
import jax.numpy as jnp
from jax import lax
from jax.experimental import pallas as pl
from jax.experimental.pallas import tpu as pltpu
from jax.sharding import PartitionSpec as P

LX = 32
LY = 16
LANES = 128
ROWS = 16
MESH = pl.DeviceIdType.MESH
F32 = jnp.float32
BF16 = jnp.bfloat16

two_pi = 2.0 * math.pi

ORDER = (
    "f0 t2 f1 F01",
    "f2 T F02 F11",
    "F03 F12 F04 F21",
    "M0 F13 F22 F14",
    "M1 F23 R0 F24",
    "M2 R1 Z0 R2",
    "X01 Z1 X02 X11",
    "Z2 X03 X12 X21",
    "X04 O0 X13 X22",
    "X14 O1 X23 X24",
    "O2 P",
)


def link_times(entry, re, im, dagger):
    out_re, out_im = [], []
    for target in range(3):
        total_re = total_im = None
        for source in range(3):
            place = source * 3 + target if dagger else target * 3 + source
            ere, eim = entry[place], entry[9 + place]
            if dagger:
                tre = ere * re[source] + eim * im[source]
                tim = ere * im[source] - eim * re[source]
            else:
                tre = ere * re[source] - eim * im[source]
                tim = ere * im[source] + eim * re[source]
            total_re = tre if total_re is None else total_re + tre
            total_im = tim if total_im is None else total_im + tim
        out_re.append(total_re)
        out_im.append(total_im)
    return out_re + out_im


def elementals(
    ring, sites, chunks, momenta_count,
    x0_hbm, links_hbm, owner_hbm, momenta_hbm, tau_hbm, out_hbm,
    x0, links, owner, momenta, tau, out, ordered, turned, lk, cs, t1, acc, out0, out1, in0, in1, weights, *rest,
):
    gathered, parts, rs_in, phi = (rest[k * chunks : (k + 1) * chunks] for k in range(4))
    loaded, stored, halo_send, halo_recv, f_send, f_recv, rs_send, rs_recv, z_send, z_recv, x_send, x_recv = rest[4 * chunks :]
    x = lax.axis_index("vec")
    z = lax.axis_index("site")
    tiles = links.shape[0] // 54
    plane = tiles * LANES
    block = chunks * ROWS
    half_ring = ring // 2
    groups = parts[0].shape[0]
    group_rows = parts[0].shape[1]

    barrier = pltpu.get_barrier_semaphore()

    def greet(d, carry):
        pl.semaphore_signal(barrier, inc=1, device_id={"site": lax.rem(z + d, sites)}, device_id_type=MESH)
        return carry

    lax.fori_loop(1, sites, greet, 0)
    for d in (1, ring - 1):
        pl.semaphore_signal(barrier, inc=1, device_id={"vec": lax.rem(x + d, ring)}, device_id_type=MESH)

    def lanes_of(t):
        return pl.ds(pl.multiple_of(t * LANES, LANES), LANES)

    def entries(hop, lanes):
        return [lk[hop * 18 + e, :, lanes][None] for e in range(18)]

    def vectors(ref, c, t):
        if ref is x0:
            return [
                x0[pl.ds((comp * block + c * ROWS) * tiles + t, ROWS, stride=tiles), :].reshape(2, 8, LANES)
                for comp in range(6)
            ]
        return [ref[comp, pl.ds(2 * c, 2), :, lanes_of(t)] for comp in range(6)]

    def pack(value):
        return value.reshape(ROWS, LANES).astype(BF16)

    def unpack(value):
        return value.astype(F32).reshape(2, 8, LANES)

    loads = [
        pltpu.make_async_copy(source, target, loaded.at[k])
        for k, (source, target) in enumerate(
            ((links_hbm, links), (x0_hbm, x0), (owner_hbm, owner), (momenta_hbm, momenta), (tau_hbm, tau))
        )
    ]
    for load in loads:
        load.start()

    spread_lane = lax.broadcasted_iota(jnp.int32, (8, LANES), 1)

    def link_row(e, t):
        return jnp.broadcast_to(links[pl.ds(e * tiles + t, 1), :], (8, LANES))

    def spread_in_plane(e, carry):
        for t in range(tiles):
            lanes = pl.ds(t * LANES, LANES)
            along_x, along_y = link_row(e, t), link_row(18 + e, t)
            before = link_row(18 + e, (t + tiles - 1) % tiles)
            lk[e, :, lanes] = along_x
            lk[18 + e, :, lanes] = jnp.where(
                spread_lane % LX == 0, pltpu.roll(along_x, LANES + 1 - LX, 1), pltpu.roll(along_x, 1, 1)
            )
            lk[36 + e, :, lanes] = along_y
            lk[54 + e, :, lanes] = jnp.where(
                spread_lane >= LX, pltpu.roll(along_y, LX, 1), pltpu.roll(before, LX, 1)
            )
        return carry

    def spread_across(e, carry):
        for t in range(tiles):
            lk[72 + e, :, pl.ds(t * LANES, LANES)] = link_row(36 + e, t)
        return carry

    def turn():
        flat = lax.broadcasted_iota(jnp.int32, (8, plane), 1)
        for p in range(momenta_count):
            theta = two_pi * (
                (momenta[p, 0] * (flat % LX)).astype(F32) / LX
                + (momenta[p, 1] * (flat // LX)).astype(F32) / LY
                + (jnp.zeros_like(flat) + momenta[p, 2] * z).astype(F32) / sites
            )
            cs[p, 0] = jnp.cos(theta)
            cs[p, 1] = jnp.sin(theta)

    lane = lax.broadcasted_iota(jnp.int32, (2, 8, LANES), 2)
    last_column = lane % LX == LX - 1
    first_column = lane % LX == 0

    def roll(value, shift):
        return pltpu.roll(value.reshape(ROWS, LANES), shift, 1).reshape(2, 8, LANES)

    def outgoing(source, out, c):
        def body(t, carry):
            lanes = lanes_of(t)
            field = vectors(source, c, t)
            sent = link_times(entries(4, lanes), field[:3], field[3:], True)
            for comp in range(6):
                out[c, 0, comp, :, lanes] = pack(field[comp])
                out[c, 1, comp, :, lanes] = pack(sent[comp])
            return carry

        lax.fori_loop(0, tiles, body, 0)

    def in_plane(source, c):
        def body(t, carry):
            lanes = lanes_of(t)
            field = vectors(source, c, t)
            ahead = [jnp.where(last_column, roll(w, LX - 1), roll(w, LANES - 1)) for w in field]
            total = link_times(entries(0, lanes), ahead[:3], ahead[3:], False)
            behind = [jnp.where(first_column, roll(w, LANES + 1 - LX), roll(w, 1)) for w in field]
            added = link_times(entries(1, lanes), behind[:3], behind[3:], True)
            total = [a + b for a, b in zip(total, added)]
            after = vectors(source, c, lax.rem(t + 1, tiles))
            ahead = [
                jnp.where(lane < LANES - LX, roll(w, LANES - LX), roll(v, LANES - LX)) for w, v in zip(field, after)
            ]
            added = link_times(entries(2, lanes), ahead[:3], ahead[3:], False)
            total = [a + b for a, b in zip(total, added)]
            before = vectors(source, c, lax.rem(t + tiles - 1, tiles))
            behind = [jnp.where(lane >= LX, roll(w, LX), roll(v, LX)) for w, v in zip(field, before)]
            added = link_times(entries(3, lanes), behind[:3], behind[3:], True)
            for comp in range(6):
                acc[comp, pl.ds(2 * c, 2), :, lanes] = total[comp] + added[comp]
            return carry

        lax.fori_loop(0, tiles, body, 0)

    def applied(c, t, arrived):
        lanes = lanes_of(t)
        total = vectors(acc, c, t)
        field = [unpack(arrived[c, 0, comp, :, lanes]) for comp in range(6)]
        added = link_times(entries(4, lanes), field[:3], field[3:], False)
        return [
            (total[comp] + added[comp] + unpack(arrived[c, 1, comp, :, lanes])) * (-1.0 / 6.0) for comp in range(6)
        ]

    up, down = lax.rem(z + 1, sites), lax.rem(z + sites - 1, sites)

    def halo(round_, c, way, target):
        out, arrived = (out0, in0) if round_ == 0 else (out1, in1)
        here, there = (out.at[c], arrived.at[c]) if way is None else (out.at[c, way], arrived.at[c, way])
        return pltpu.make_async_remote_copy(
            src_ref=here, dst_ref=there,
            send_sem=halo_send.at[round_, c], recv_sem=halo_recv.at[round_, c],
            device_id={"site": target}, device_id_type=MESH,
        )

    def send_halo(round_, c):
        halo(round_, c, 0, down).start()
        halo(round_, c, 1, up).start()

    def first_step(c):
        halo(0, c, None, up).wait_recv()

        def first(t, carry):
            lanes = lanes_of(t)
            result = applied(c, t, in0)
            sent = link_times(entries(4, lanes), result[:3], result[3:], True)
            for comp in range(6):
                t1[comp, pl.ds(2 * c, 2), :, lanes] = result[comp]
                out1[c, 0, comp, :, lanes] = pack(result[comp])
                out1[c, 1, comp, :, lanes] = pack(sent[comp])
            return carry

        lax.fori_loop(0, tiles, first, 0)
        send_halo(1, c)

    loads[0].wait()
    lax.fori_loop(0, 18, spread_across, 0)
    loads[1].wait()
    outgoing(x0, out0, 0)
    pl.semaphore_wait(barrier, sites - 1 + 2)
    send_halo(0, 0)
    for c in range(1, chunks):
        outgoing(x0, out0, c)
        if c == 1:
            send_halo(0, c)
    lax.fori_loop(0, 18, spread_in_plane, 0)
    in_plane(x0, 0)
    first_step(0)
    for c in range(2, chunks):
        send_halo(0, c)
    in_plane(t1, 0)
    in_plane(x0, 1)
    first_step(1)
    in_plane(t1, 1)
    in_plane(x0, 2)
    for load in loads[2:]:
        load.wait()
    turn()

    vectors_ring = (gathered, 3, 2, f_send, f_recv)
    phi_ring = (phi, phi[0].shape[1] // 2, 1, x_send, x_recv)

    def ring_copies(which, c, step, source_step):
        buffers, span, pieces, sends, recvs = which
        for piece in range(pieces if step < half_ring else 1):
            for way in range(2):
                if step == half_ring:
                    part = pl.ds(way * span, span)
                elif pieces == 2:
                    part = pl.ds(piece * span, span)
                else:
                    part = pl.ds(0, 2 * span)
                back_by = (ring - source_step) % ring if way == 0 else source_step
                here = buffers[c].at[lax.rem(x + back_by, ring), part]
                yield pltpu.make_async_remote_copy(
                    src_ref=here, dst_ref=here,
                    send_sem=sends.at[c], recv_sem=recvs.at[c, ((step - 1) * pieces + piece) * 2 + way],
                    device_id={"vec": lax.rem(x + (1 if way == 0 else ring - 1), ring)}, device_id_type=MESH,
                )

    def start_ring(which, c):
        for copy in ring_copies(which, c, 1, 0):
            copy.start()

    def ring_forward(which, c, step):
        passed_on = list(ring_copies(which, c, step + 1, step)) if step < half_ring else []
        for number, copy in enumerate(ring_copies(which, c, step, step)):
            copy.wait_recv()
            if step + 1 < half_ring:
                passed_on[number].start()
            elif step < half_ring and which[2] == 2 and number in (0, 3):
                passed_on[number // 2].start()
            elif step < half_ring and which[2] == 1:
                passed_on[number].start()

    def ring_sent(which, c):
        buffers, span, pieces, sends, recvs = which
        whole = buffers[c].at[pl.ds(0, ring - 1)]
        pltpu.make_async_remote_copy(
            src_ref=whole, dst_ref=whole, send_sem=sends.at[c], recv_sem=recvs.at[c, 0],
            device_id={"vec": lax.rem(x + 1, ring)}, device_id_type=MESH,
        ).wait_send()

    def filter_chunk(c):
        halo(1, c, None, up).wait_recv()

        def second(t, carry):
            lanes = lanes_of(t)
            result = applied(c, t, in1)
            start = vectors(x0, c, t)
            for comp in range(6):
                gathered[c][x, comp, :, lanes] = pack(2.0 * result[comp] - start[comp])
            return carry

        lax.fori_loop(0, tiles, second, 0)
        start_ring(vectors_ring, c)

        def phases(t, carry):
            lanes = lanes_of(t)
            for color in range(3):
                re = unpack(gathered[c][x, color, :, lanes])
                im = unpack(gathered[c][x, 3 + color, :, lanes])
                for p in range(momenta_count):
                    cosine, sine = cs[p, 0, :, lanes][None], cs[p, 1, :, lanes][None]
                    shift_re = pack(cosine * re + sine * im)
                    shift_im = pack(cosine * im - sine * re)
                    real = pl.ds(2 * p * block + c * ROWS, ROWS)
                    imag = pl.ds((2 * p + 1) * block + c * ROWS, ROWS)
                    weights[color, real, lanes] = shift_re
                    weights[3 + color, real, lanes] = shift_im
                    weights[color, imag, lanes] = shift_im
                    weights[3 + color, imag, lanes] = -shift_re
            return carry

        lax.fori_loop(0, tiles, phases, 0)

    inverse = []
    for place in range(ring):
        found = 0
        for b in range(ring):
            found = jnp.where(owner[b] == place, b, found)
        inverse.append(found)

    def group_of(device):
        index = (device * groups + sites - 1) // sites
        return index, jnp.logical_and(index < groups, (index * sites) // groups == device)

    my_group, reduces = group_of(z)
    spare = jnp.where(reduces, my_group, 0)

    def far_first(i):
        k = (i + 1) // 2
        return sites // 2 + jnp.where(i % 2 == 0, k, -k)

    def to_plane(c, here, there, send, recv, target):
        return pltpu.make_async_remote_copy(
            src_ref=here, dst_ref=there, send_sem=send.at[c], recv_sem=recv.at[c],
            device_id={"site": target}, device_id_type=MESH,
        )

    def multiply(c):
        total = None
        for comp in range(6):
            left = weights[comp]
            right = jnp.concatenate([gathered[c][inverse[place], comp] for place in range(ring)], axis=0)
            product = lax.dot_general(left, right, (((1,), (1,)), ((), ())), preferred_element_type=F32)
            total = product if total is None else total + product
        parts[c][...] = total.reshape(groups, group_rows, ring * ROWS).astype(BF16)

        def send(i, carry):
            away = far_first(i)
            target = lax.rem(z + away, sites)
            group, valid = group_of(target)

            @pl.when(valid)
            def _():
                to_plane(
                    c, parts[c].at[group], rs_in[c].at[sites - 1 - away], rs_send, rs_recv, target
                ).start()

            return carry

        lax.fori_loop(0, sites - 1, send, 0)

    def rows_of(group, count=1):
        return pl.ds(pl.multiple_of(group * group_rows, ROWS), count * group_rows)

    def reduce(c):
        @pl.when(reduces)
        def _():
            to_plane(c, rs_in[c], rs_in[c], rs_send, rs_recv, up).wait_recv()

            def add(i, total):
                return total + rs_in[c][i].astype(F32)

            total = lax.fori_loop(0, sites - 1, add, parts[c][spare].astype(F32))
            phi[c][x, rows_of(spare), :] = total.astype(BF16)
            mine = phi[c].at[x, rows_of(spare)]

            def send(i, carry):
                to_plane(c, mine, mine, z_send, z_recv, lax.rem(z + far_first(i), sites)).start()
                return carry

            lax.fori_loop(0, sites - 1, send, 0)

    def gather_planes(c):
        @pl.when(reduces)
        def _():
            others = phi[c].at[x, rows_of(0, groups - 1)]
            to_plane(c, others, others, z_send, z_recv, up).wait_recv()

        @pl.when(jnp.logical_not(reduces))
        def _():
            others = phi[c].at[x, rows_of(0, groups)]
            to_plane(c, others, others, z_send, z_recv, up).wait_recv()

        start_ring(phi_ring, c)

    def all_sent(c):
        halo(0, c, None, up).wait_send()
        halo(1, c, None, up).wait_send()
        ring_sent(vectors_ring, c)
        ring_sent(phi_ring, c)

        @pl.when(reduces)
        def _():
            others = parts[c].at[pl.ds(0, groups - 1)]
            to_plane(c, others, others, rs_send, rs_recv, up).wait_send()
            to_plane(c, rs_in[c], rs_in[c], z_send, z_recv, up).wait_send()

        @pl.when(jnp.logical_not(reduces))
        def _():
            to_plane(c, parts[c], parts[c], rs_send, rs_recv, up).wait_send()

    width = ring * block
    piece = ring * ROWS
    outer = tau.shape[0]

    def turn_tau():
        row = lax.broadcasted_iota(jnp.int32, (width, width), 0)
        spot = lax.broadcasted_iota(jnp.int32, (width, width), 1)
        origin = ((spot % piece) // ROWS) * block + (spot // piece) * ROWS + spot % ROWS
        swap = jnp.where(row == origin, 1.0, 0.0).astype(BF16)
        for part in range(2):
            rows = tau[:, part].reshape(outer * block, width)
            turned[part] = jnp.dot(rows, swap, preferred_element_type=F32).astype(BF16)
        turned[2] = -turned[1]

    def order(c):
        for place in range(ring):
            ordered[:, place * block : (place + 1) * block, c * piece : (c + 1) * piece] = phi[c][
                inverse[place]
            ].reshape(2 * momenta_count, block, piece)

    def times(a, p, b):
        return lax.dot_general(turned[a], ordered[2 * p + b], (((1,), (1,)), ((), ())), preferred_element_type=F32)

    def project():
        stores = []
        for p in range(momenta_count):
            real = times(0, p, 0) + times(2, p, 1)
            out[:, p, 0] = real.astype(BF16).reshape(outer, block, width)
            imag = times(0, p, 1) + times(1, p, 0)
            out[:, p, 1] = imag.astype(BF16).reshape(outer, block, width)
            stores.append(pltpu.make_async_copy(out.at[:, p], out_hbm.at[:, p], stored.at[p]))
            stores[p].start()
        for store in stores:
            store.wait()

    for op in " ".join(ORDER).split():
        c, step = int(op[1:2] or 0), int(op[2:] or 0)
        if step > half_ring:
            continue
        if op[0] == "f":
            filter_chunk(c)
        elif op[0] == "T":
            turn_tau()
        elif op[0] == "O":
            order(c)
        elif op[0] == "P":
            project()
        elif op[0] == "t":
            first_step(c)
            in_plane(t1, c)
        elif op[0] == "F":
            ring_forward(vectors_ring, c, step)
        elif op[0] == "M":
            multiply(c)
        elif op[0] == "R":
            reduce(c)
        elif op[0] == "Z":
            gather_planes(c)
        else:
            ring_forward(phi_ring, c, step)
    for c in range(chunks):
        all_sent(c)


def per_device(eigvecs, links, peramb, block_owner, momenta):
    ring, sites = lax.axis_size("vec"), lax.axis_size("site")
    block = eigvecs.shape[3]
    plane = eigvecs.shape[5]
    chunks = block // ROWS
    momenta_count = momenta.shape[0]
    rows = 2 * momenta_count * block
    groups = max(g for g in range(1, sites + 1) if (rows // ROWS) % g == 0)
    group_rows = rows // groups
    piece = ring * ROWS
    half_ring = ring // 2
    x0 = eigvecs.reshape(-1, LANES)
    table = links.reshape(-1, LANES)
    anywhere = pl.BlockSpec(memory_space=pl.ANY)
    packed = pltpu.VMEM((chunks, 2, 6, ROWS, plane), BF16)
    field = pltpu.VMEM((6, block // 8, 8, plane), F32)
    dma = pltpu.SemaphoreType.DMA
    sinks, spins = peramb.shape[1], peramb.shape[2]
    width = ring * block
    tau = peramb.reshape(sinks * spins, 2, block, width)
    out = jax.ShapeDtypeStruct((sinks * spins, momenta_count, 2, block, width), BF16)
    result = pl.pallas_call(
        functools.partial(elementals, ring, sites, chunks, momenta_count),
        out_shape=out,
        in_specs=[anywhere] * 5,
        out_specs=anywhere,
        scratch_shapes=[
            pltpu.VMEM(x0.shape, F32),
            pltpu.VMEM(table.shape, F32),
            pltpu.SMEM(block_owner.shape, jnp.int32),
            pltpu.SMEM(momenta.shape, jnp.int32),
            pltpu.VMEM(tau.shape, BF16),
            pltpu.VMEM(out.shape, BF16),
            pltpu.VMEM((2 * momenta_count, width, width), BF16),
            pltpu.VMEM((3, sinks * spins * block, width), BF16),
            pltpu.VMEM((90, 8, plane), F32),
            pltpu.VMEM((momenta_count, 2, 8, plane), F32),
            field,
            field,
            *[packed] * 4,
            pltpu.VMEM((6, rows, plane), BF16),
            *[pltpu.VMEM((ring, 6, ROWS, plane), BF16)] * chunks,
            *[pltpu.VMEM((groups, group_rows, piece), BF16)] * chunks,
            *[pltpu.VMEM((sites - 1, group_rows, piece), BF16)] * chunks,
            *[pltpu.VMEM((ring, rows, piece), BF16)] * chunks,
            dma((5,)),
            dma((momenta_count,)),
            dma((2, chunks)),
            dma((2, chunks)),
            dma((chunks,)),
            dma((chunks, 4 * half_ring - 2)),
            dma((chunks,)),
            dma((chunks,)),
            dma((chunks,)),
            dma((chunks,)),
            dma((chunks,)),
            dma((chunks, 2 * half_ring)),
        ],
        compiler_params=pltpu.CompilerParams(collective_id=0, has_side_effects=True),
        name="elementals",
    )(x0, table, block_owner, momenta, tau)
    return result.reshape(1, sinks, spins, momenta_count, 2, block, width)


def solution(mesh):
    placed = (
        P(("cfg", "tslice"), None, None, "vec", "site", None),
        P(("cfg", "tslice"), None, None, None, None, "site", None),
        P(("cfg", "tslice"), "site", None, None, "vec", None),
        P(),
        P(),
    )
    return jax.shard_map(
        per_device,
        mesh=mesh,
        in_specs=placed,
        out_specs=P(("cfg", "tslice"), "site", None, None, None, "vec", None),
        check_vma=False,
    )
```

time: 133 us -> 123 us (0.925)
  Pallas kernels: 129 us -> 121 us
    pallas_call x1 -> x0, Pallas kernels: 4.52 us -> none  [per_device(): pl.pallas_call(functools.partial(project, ring, chunks, momenta_count), o...]
    pallas_call x1, Pallas kernels: 125 us -> 121 us  [per_device(): pl.pallas_call(functools.partial(elementals, ring, sites, chunks, momenta...]
where the time goes in v2:
time: 123 us
  Pallas kernels  121 us (98%)
  local copies, waits for them, and re-layouts  2.4 us (2%)
    pallas_call x1, Pallas kernels, per_device(): pl.pallas_call(functools.partial(elementals, ring, sites, chunks, momenta...  121 us

profile of v2, /device:TPU:80, one launch (start us, length us, event | category | flops | bytes accessed | tf_op | source)
XLA Modules:
  0.0 123.0 jit_solution(682206762359052478)
XLA Ops:
  0.0 120.6 %elementals.1 = bf16[8,2,2,48,384]{4,3,2,1,0:T(8,128)(2,1)} custom-call(f32[1152,128]{1,0:T(8,128)} %bitcast.5, f32[216,128]{1,0:T(8,128)} %bitcast.7, s32[8]{0:T(128)} %owner_hbm.1, s32[2,3]{1,0:T(2,128)} %momenta_hbm.1, bf16[8,2,48,384]{3,2,1,0:T(8,128)(2,1)} %bitcast.6), custom_call_target="tpu_custom_call" | custom-call | tf_op jit(solution)/shard_map/elementals/pallas_call | solution.py:514
  120.6 2.4 %copy.7 = bf16[1,2,4,2,2,48,384]{6,5,4,3,2,1,0:T(8,128)(2,1)} copy(bf16[1,2,4,2,2,48,384]{6,5,4,3,2,1,0:T(8,128)(2,1)} %bitcast.4) | data formatting | bytes 2359296
